TPU v7x, 32 devices: a whole 2x2x4 slice. The times are simulated.
32 devices in a mesh: row: 4 (over z), col: 4 (over y, core), rep: 2 (over x).
Axes of the slice: x: 2, y: 2, z: 4, core: 2. Of those that a mesh axis runs over, the one named last changes fastest.
Arguments:
- amplitudes: bfloat16 [1024, 8192], P('row', 'col'), may hold values from -6 to 6
- intermediate: bfloat16 [8192, 1024], P('row', 'col'), may hold values from -0.0625 to 0.0625
Outputs:
- residual: float32 [8, 4, 32, 1024], P(None, 'col', None, ('row', 'rep'))
All inputs are finite; a program needn't handle non-finite values.
Results may differ from a plain program's by a relative error of at most 0.0029.
Values may be sent and summed in bfloat16 or wider, within the bound.
A program may use at most 128 MiB of HBM per device.

v0:
```python
import jax
import jax.numpy as jnp
from jax import lax
from jax.sharding import PartitionSpec as P


def local(amplitudes, intermediate):
    rows_axis = lax.axis_size("row")
    cols_axis = lax.axis_size("col")
    depth_axis = lax.axis_size("rep")
    layer_index = lax.axis_index("rep")
    owner_rows = rows_axis * depth_axis
    fold_count = owner_rows // cols_axis
    local_rows = amplitudes.shape[0]
    band_rows = local_rows // depth_axis
    local_cols = intermediate.shape[1]
    slice_width = local_cols // owner_rows
    own_rows = lax.dynamic_slice_in_dim(amplitudes, layer_index * band_rows, band_rows, 0)
    all_weights = lax.all_gather(intermediate, "row", axis=0, tiled=True)
    summed = jnp.dot(
        lax.all_gather(own_rows, "col", axis=1, tiled=True),
        all_weights,
        preferred_element_type=jnp.float32,
    )
    cycle = summed.astype(jnp.bfloat16)
    spread_block = cycle.reshape(band_rows, fold_count, cols_axis, slice_width)
    direct = lax.all_to_all(spread_block, "col", split_axis=2, concat_axis=1, tiled=True).reshape(
        band_rows, owner_rows, slice_width
    )
    stacked = cycle.reshape(cols_axis, slice_width, fold_count, cols_axis * slice_width)
    mirror = lax.all_to_all(
        lax.all_to_all(stacked, "col", split_axis=0, concat_axis=2, tiled=True),
        ("row", "rep"),
        split_axis=2,
        concat_axis=0,
        tiled=True,
    )
    mirror_part = mirror.reshape(owner_rows, slice_width, band_rows).astype(jnp.float32)
    direct_part = jnp.transpose(direct, (1, 2, 0)).astype(jnp.float32)
    return (mirror_part + direct_part).reshape(owner_rows, 1, slice_width, band_rows)


def solution(mesh):
    in_specs = (P("row", "col"), P("row", "col"))
    out_specs = P(None, "col", None, ("row", "rep"))
    return jax.shard_map(local, mesh=mesh, in_specs=in_specs, out_specs=out_specs, check_vma=False)
```

profile of v0, /device:TPU:0, one launch (start us, length us, event | category | flops | bytes accessed | tf_op | source)
XLA Modules:
  0.0 153.2 jit_solution(1492077100807773133)
XLA Ops:
  6.5 0.0 copy-start
  6.5 0.0 all-gather.3.cloned.1.call-start
  6.5 1.2 copy-done
  7.8 0.9 constant_dynamic-slice_fusion
  8.6 0.0 all-gather.3.cloned.1.call-update
  8.6 0.0 all-gather.5.cloned.1.call-start
  8.7 0.7 all-gather.5.cloned.1.call-update
  9.4 24.8 %all-gather.3.cloned.1.call-done = bf16[128,8192]{1,0:T(8,128)(2,1)} async-done(((bf16[128,2048]{1,0:T(8,128)(2,1)}), bf16[128,8192]{1,0:T(8,128)(2,1)}) %all-gather.3.cloned.1.call-update) | async-done | bytes 2097168 | tf_op jit(solution)/shard_map/all_gather | solution.py:21
  34.2 82.3 %all-gather.5.cloned.1.call-done = bf16[8192,256]{1,0:T(8,128)(2,1)} async-done(((bf16[2048,256]{1,0:T(8,128)(2,1)}), bf16[8192,256]{1,0:T(8,128)(2,1)}) %all-gather.5.cloned.1.call-update) | async-done | bytes 4194320 | tf_op jit(solution)/shard_map/all_gather | solution.py:19
  116.6 3.5 %convolution_convert_fusion = bf16[128,256]{1,0:T(8,128)(2,1)S(1)} fusion(bf16[128,8192]{1,0:T(8,128)(2,1)} %all-gather.3.cloned.1.call-done, bf16[8192,256]{1,0:T(8,128)(2,1)} %all-gather.5.cloned.1.call-done), kind=kOutput, calls=%fused_computation | convolution fusion | flops 536903680 | bytes 6356992 | tf_op jit(solution)/shard_map/dot_general | solution.py:20
  120.1 0.7 reshape.21
  120.7 3.3 %all-to-all-start = ((bf16[4,32,2,128]{3,2,1,0:T(2,128)(2,1)}), bf16[4,32,2,128]{3,2,1,0:T(2,128)(2,1)S(1)}, u32[]{:S(2)}, u32[]{:S(2)}) async-start(bf16[4,32,2,128]{3,2,1,0:T(2,128)(2,1)} %reshape.21), calls=%async_computation | async-start | bytes 131072 | tf_op jit(solution)/shard_map/all_to_all | solution.py:32
  124.0 0.1 copy.13
  124.2 0.6 copy.14
  124.8 3.3 %all-to-all-done = bf16[4,32,2,128]{3,2,1,0:T(2,128)(2,1)S(1)} async-done(((bf16[4,32,2,128]{3,2,1,0:T(2,128)(2,1)}), bf16[4,32,2,128]{3,2,1,0:T(2,128)(2,1)S(1)}, u32[]{:S(2)}, u32[]{:S(2)}) %all-to-all-start) | async-done | bytes 65568 | tf_op jit(solution)/shard_map/all_to_all | solution.py:32
  128.1 3.3 %all-to-all-start.2 = ((bf16[128,2,4,32]{0,3,1,2:T(8,128)(2,1)}), bf16[128,2,4,32]{0,3,1,2:T(8,128)(2,1)S(1)}, u32[]{:S(2)}, u32[]{:S(2)}) async-start(bf16[128,2,4,32]{0,3,1,2:T(8,128)(2,1)} %copy.14), calls=%async_computation.2 | async-start | bytes 131072 | tf_op jit(solution)/shard_map/all_to_all | solution.py:27
  131.4 0.6 copy.11
  132.1 3.4 %all-to-all-done.2 = bf16[128,2,4,32]{0,3,1,2:T(8,128)(2,1)S(1)} async-done(((bf16[128,2,4,32]{0,3,1,2:T(8,128)(2,1)}), bf16[128,2,4,32]{0,3,1,2:T(8,128)(2,1)S(1)}, u32[]{:S(2)}, u32[]{:S(2)}) %all-to-all-start.2) | async-done | bytes 65568 | tf_op jit(solution)/shard_map/all_to_all | solution.py:27
  135.5 3.3 %all-to-all-start.1 = ((bf16[1,32,8,128]{3,1,0,2:T(8,128)(2,1)}), bf16[1,32,8,128]{3,1,0,2:T(8,128)(2,1)S(1)}, u32[]{:S(2)}, u32[]{:S(2)}) async-start(bf16[1,32,8,128]{3,1,0,2:T(8,128)(2,1)} %bitcast.2), calls=%async_computation.1 | async-start | bytes 131072 | tf_op jit(solution)/shard_map/all_to_all | solution.py:31
  138.9 6.8 %all-to-all-done.1 = bf16[1,32,8,128]{3,1,0,2:T(8,128)(2,1)S(1)} async-done(((bf16[1,32,8,128]{3,1,0,2:T(8,128)(2,1)}), bf16[1,32,8,128]{3,1,0,2:T(8,128)(2,1)S(1)}, u32[]{:S(2)}, u32[]{:S(2)}) %all-to-all-start.1) | async-done | bytes 65568 | tf_op jit(solution)/shard_map/all_to_all | solution.py:31
  145.7 0.7 bitcast_add_fusion
  (1 shorter events, 0.0 us)
Async XLA Ops:
  6.5 1.2 copy-start
  6.5 27.7 %all-gather.3.cloned.1.call-start = ((), (), s32[]{:S(2)}) async-start(), calls=%async_computation.3 | async-start | bytes 2621440 | tf_op jit(solution)/shard_map/all_gather | solution.py:21
  8.6 107.9 %all-gather.5.cloned.1.call-start = ((), (), s32[]{:S(2)}) async-start(), calls=%async_computation.4 | async-start | bytes 5242880 | tf_op jit(solution)/shard_map/all_gather | solution.py:19
  120.7 7.4 %all-to-all-start = ((bf16[4,32,2,128]{3,2,1,0:T(2,128)(2,1)}), bf16[4,32,2,128]{3,2,1,0:T(2,128)(2,1)S(1)}, u32[]{:S(2)}, u32[]{:S(2)}) async-start(bf16[4,32,2,128]{3,2,1,0:T(2,128)(2,1)} %reshape.21), calls=%async_computation | async-start | bytes 131072 | tf_op jit(solution)/shard_map/all_to_all | solution.py:32
  128.1 7.4 %all-to-all-start.2 = ((bf16[128,2,4,32]{0,3,1,2:T(8,128)(2,1)}), bf16[128,2,4,32]{0,3,1,2:T(8,128)(2,1)S(1)}, u32[]{:S(2)}, u32[]{:S(2)}) async-start(bf16[128,2,4,32]{0,3,1,2:T(8,128)(2,1)} %copy.14), calls=%async_computation.2 | async-start | bytes 131072 | tf_op jit(solution)/shard_map/all_to_all | solution.py:27
  135.5 10.2 %all-to-all-start.1 = ((bf16[1,32,8,128]{3,1,0,2:T(8,128)(2,1)}), bf16[1,32,8,128]{3,1,0,2:T(8,128)(2,1)S(1)}, u32[]{:S(2)}, u32[]{:S(2)}) async-start(bf16[1,32,8,128]{3,1,0,2:T(8,128)(2,1)} %bitcast.2), calls=%async_computation.1 | async-start | bytes 131072 | tf_op jit(solution)/shard_map/all_to_all | solution.py:31
Sparse Core Ops, SparseCore 0:
  8.9 25.2 all-gather.2
  35.8 80.7 all-gather.4
where the time goes:
time: 154 us; the launch traced here: 153 us
  waiting for transfers between devices  121 us (79%)
  between operations  13.4 us (9%)
  starting transfers between devices  9.96 us (6%)
  local copies, waits for them, and re-layouts  4.12 us (3%)
  matrix products  3.53 us (2%)
    all_gather x1, waiting for transfers between devices, local(): all_weights = lax.all_gather(intermediate, 'row', axis=0, tiled=True)  82.3 us
    all_gather x1, waiting for transfers between devices, local(): lax.all_gather(own_rows, 'col', axis=1, tiled=True)  24.8 us
    all_to_all x1, waiting for transfers between devices, local(): lax.all_to_all(lax.all_to_all(stacked, 'col', split_axis=0, concat_axis=2...  6.82 us
    dot_general x1, matrix products, local(): jnp.dot(lax.all_gather(own_rows, 'col', axis=1, tiled=True), all_weights,...  3.53 us
    all_to_all x1, waiting for transfers between devices, local(): lax.all_to_all(spread_block, 'col', split_axis=2, concat_axis=1, tiled=True)  3.44 us
    all_to_all x1, starting transfers between devices, local(): lax.all_to_all(lax.all_to_all(stacked, 'col', split_axis=0, concat_axis=2...  3.35 us
    all_to_all x1, waiting for transfers between devices, local(): lax.all_to_all(stacked, 'col', split_axis=0, concat_axis=2, tiled=True)  3.33 us
    all_to_all x1, starting transfers between devices, local(): lax.all_to_all(spread_block, 'col', split_axis=2, concat_axis=1, tiled=True)  3.29 us
  transfers between devices with their start and end apart: 5, of which 5 were waited for; matrix products, arithmetic and copies ran while one was open for 1% of the time, Pallas kernels for 0%

commit v1 on v0

--- a/solution.py
+++ b/solution.py
@@ -16,7 +16,14 @@
     local_cols = intermediate.shape[1]
     slice_width = local_cols // owner_rows
     own_rows = lax.dynamic_slice_in_dim(amplitudes, layer_index * band_rows, band_rows, 0)
-    all_weights = lax.all_gather(intermediate, "row", axis=0, tiled=True)
+    size = lax.axis_size("row")
+    forward = [(i, (i + 1) % size) for i in range(size)]
+    parts = [intermediate]
+    for hop in range(1, size):
+        parts = [lax.ppermute(parts[0], "row", forward), *parts]
+    result = jnp.concatenate(parts, axis=0)
+    turn = (lax.axis_index("row") + 1) * parts[-1].shape[0]
+    all_weights = jnp.roll(result, turn, axis=0)
     summed = jnp.dot(
         lax.all_gather(own_rows, "col", axis=1, tiled=True),
         all_weights,

time: 154 us -> 137 us (0.89)
  waiting for transfers between devices: 121 us -> 89.9 us
  local copies, waits for them, and re-layouts: 4.12 us -> 16.3 us
  starting transfers between devices: 9.96 us -> 13 us
    all_gather x1 -> x0, waiting for transfers between devices: 82.3 us -> none  [local(): all_weights = lax.all_gather(intermediate, 'row', axis=0, tiled=True)]
    ppermute x0 -> x3, waiting for transfers between devices: none -> 76.3 us  [local(): parts = [lax.ppermute(parts[0], 'row', forward), *parts]]
    all_gather x1, waiting for transfers between devices: 24.8 us -> 0.01 us  [local(): lax.all_gather(own_rows, 'col', axis=1, tiled=True)]
    unnamed x2 -> x11, local copies, waits for them, and re-layouts: 1.22 us -> 12.3 us
    ppermute x0 -> x3, starting transfers between devices: none -> 3.06 us  [local(): parts = [lax.ppermute(parts[0], 'row', forward), *parts]]
  transfers between devices with their start and end apart: 5 -> 7, of which waited for: 5 -> 6; matrix products, arithmetic and copies ran while one was open for 1% -> 11% of each run, Pallas kernels for 0% -> 0%
where the time goes in v1:
time: 137 us
  waiting for transfers between devices  89.9 us (66%)
  local copies, waits for them, and re-layouts  16.3 us (12%)
  between operations  13.4 us (10%)
  starting transfers between devices  13 us (9%)
  matrix products  3.54 us (3%)
    ppermute x3, waiting for transfers between devices, local(): parts = [lax.ppermute(parts[0], 'row', forward), *parts]  76.3 us
    unnamed x11, local copies, waits for them, and re-layouts  12.3 us
    all_to_all x1, waiting for transfers between devices, local(): lax.all_to_all(lax.all_to_all(stacked, 'col', split_axis=0, concat_axis=2...  6.82 us
    dot_general x1, matrix products, local(): jnp.dot(lax.all_gather(own_rows, 'col', axis=1, tiled=True), all_weights,...  3.54 us
    all_to_all x1, waiting for transfers between devices, local(): lax.all_to_all(spread_block, 'col', split_axis=2, concat_axis=1, tiled=True)  3.45 us
    all_to_all x1, starting transfers between devices, local(): lax.all_to_all(lax.all_to_all(stacked, 'col', split_axis=0, concat_axis=2...  3.35 us
    all_to_all x1, waiting for transfers between devices, local(): lax.all_to_all(stacked, 'col', split_axis=0, concat_axis=2, tiled=True)  3.33 us
    all_to_all x1, starting transfers between devices, local(): lax.all_to_all(spread_block, 'col', split_axis=2, concat_axis=1, tiled=True)  3.29 us
  transfers between devices with their start and end apart: 7, of which 6 were waited for; matrix products, arithmetic and copies ran while one was open for 11% of the time, Pallas kernels for 0%

profile of v1, /device:TPU:0, one launch (start us, length us, event | category | flops | bytes accessed | tf_op | source)
XLA Modules:
  0.0 136.8 jit_solution(8312864040941240841)
XLA Ops:
  6.5 0.0 copy-start
  6.5 0.0 copy-start.1
  6.5 0.0 all-gather.2.cloned.1.call-start
  6.5 3.1 %collective-permute-start = (bf16[2048,256]{1,0:T(8,128)(2,1)}, bf16[2048,256]{1,0:T(8,128)(2,1)S(1)}, u32[]{:S(2)}, u32[]{:S(2)}) collective-permute-start(bf16[2048,256]{1,0:T(8,128)(2,1)} %param.3), channel_id=1, source_target_pairs={{0,8},{8,16},{16,24},{24,0},{1,9},{9,17},{17,25},{25,1},{2,10},{10... | collective-permute-start | bytes 3145736 | tf_op jit(solution)/shard_map/ppermute | solution.py:23
  9.6 25.4 %collective-permute-done = bf16[2048,256]{1,0:T(8,128)(2,1)S(1)} collective-permute-done((bf16[2048,256]{1,0:T(8,128)(2,1)}, bf16[2048,256]{1,0:T(8,128)(2,1)S(1)}, u32[]{:S(2)}, u32[]{:S(2)}) %collective-permute-start) | collective-permute-done | bytes 1048608 | tf_op jit(solution)/shard_map/ppermute | solution.py:23
  35.0 0.0 collective-permute-start.1
  35.0 0.0 copy-done
  35.0 0.9 constant_dynamic-slice_fusion
  35.9 0.0 all-gather.2.cloned.1.call-update
  35.9 25.3 %collective-permute-done.1 = bf16[2048,256]{1,0:T(8,128)(2,1)} collective-permute-done((bf16[2048,256]{1,0:T(8,128)(2,1)S(1)}, bf16[2048,256]{1,0:T(8,128)(2,1)}, u32[]{:S(2)}, u32[]{:S(2)}) %collective-permute-start.1) | collective-permute-done | bytes 1048608 | tf_op jit(solution)/shard_map/ppermute | solution.py:23
  61.2 0.0 collective-permute-start.2
  61.2 25.6 %collective-permute-done.2 = bf16[2048,256]{1,0:T(8,128)(2,1)} collective-permute-done((bf16[2048,256]{1,0:T(8,128)(2,1)}, bf16[2048,256]{1,0:T(8,128)(2,1)}, u32[]{:S(2)}, u32[]{:S(2)}) %collective-permute-start.2) | collective-permute-done | bytes 1048608 | tf_op jit(solution)/shard_map/ppermute | solution.py:23
  86.8 2.3 %constant_dynamic-update-slice_fusion.7 = bf16[16384,256]{1,0:T(8,128)(2,1)} fusion(bf16[2048,256]{1,0:T(8,128)(2,1)} %collective-permute-done.2), kind=kLoop, calls=%fused_computation.12 | loop fusion | bytes 2097152
  89.1 2.3 %constant_dynamic-update-slice_fusion.6 = bf16[16384,256]{1,0:T(8,128)(2,1)} fusion(bf16[16384,256]{1,0:T(8,128)(2,1)} %constant_dynamic-update-slice_fusion.7, bf16[2048,256]{1,0:T(8,128)(2,1)} %collective-permute-done.1), kind=kLoop, calls=%fused_computation.11 | loop fusion | bytes 2097152
  91.4 1.0 constant_dynamic-update-slice_fusion.5
  92.4 0.0 copy-done.1
  92.4 1.1 constant_dynamic-update-slice_fusion.4
  93.5 2.3 %constant_dynamic-update-slice_fusion.3 = bf16[16384,256]{1,0:T(8,128)(2,1)} fusion(bf16[16384,256]{1,0:T(8,128)(2,1)} %constant_dynamic-update-slice_fusion.4, bf16[2048,256]{1,0:T(8,128)(2,1)} %collective-permute-done.2), kind=kLoop, calls=%fused_computation.8 | loop fusion | bytes 2097152
  95.7 2.3 %constant_dynamic-update-slice_fusion.2 = bf16[16384,256]{1,0:T(8,128)(2,1)} fusion(bf16[16384,256]{1,0:T(8,128)(2,1)} %constant_dynamic-update-slice_fusion.3, bf16[2048,256]{1,0:T(8,128)(2,1)} %collective-permute-done.1), kind=kLoop, calls=%fused_computation.7 | loop fusion | bytes 2097152
  98.0 1.1 constant_dynamic-update-slice_fusion.1
  99.1 1.1 constant_dynamic-update-slice_fusion
  100.2 0.0 all-gather.2.cloned.1.call-done
  100.2 3.5 %fusion.2 = bf16[128,256]{1,0:T(8,128)(2,1)S(1)} fusion(bf16[128,8192]{1,0:T(8,128)(2,1)} %all-gather.2.cloned.1.call-done, bf16[16384,256]{1,0:T(8,128)(2,1)} %constant_dynamic-update-slice_fusion, s32[]{:T(128)S(6)} %select_n.18), kind=kOutput, calls=%fused_computation.2 | convolution fusion | flops 536903680 | bytes 6356996 | tf_op jit(solution)/shard_map/dot_general | solution.py:27
  103.7 0.6 reshape.21
  104.4 3.3 %all-to-all-start = ((bf16[4,32,2,128]{3,2,1,0:T(2,128)(2,1)}), bf16[4,32,2,128]{3,2,1,0:T(2,128)(2,1)S(1)}, u32[]{:S(2)}, u32[]{:S(2)}) async-start(bf16[4,32,2,128]{3,2,1,0:T(2,128)(2,1)} %reshape.21), calls=%async_computation | async-start | bytes 131072 | tf_op jit(solution)/shard_map/all_to_all | solution.py:39
  107.7 0.1 copy.13
  107.8 0.6 copy.14
  108.4 3.3 %all-to-all-done = bf16[4,32,2,128]{3,2,1,0:T(2,128)(2,1)S(1)} async-done(((bf16[4,32,2,128]{3,2,1,0:T(2,128)(2,1)}), bf16[4,32,2,128]{3,2,1,0:T(2,128)(2,1)S(1)}, u32[]{:S(2)}, u32[]{:S(2)}) %all-to-all-start) | async-done | bytes 65568 | tf_op jit(solution)/shard_map/all_to_all | solution.py:39
  111.7 3.3 %all-to-all-start.2 = ((bf16[128,2,4,32]{0,3,1,2:T(8,128)(2,1)}), bf16[128,2,4,32]{0,3,1,2:T(8,128)(2,1)S(1)}, u32[]{:S(2)}, u32[]{:S(2)}) async-start(bf16[128,2,4,32]{0,3,1,2:T(8,128)(2,1)} %copy.14), calls=%async_computation.2 | async-start | bytes 131072 | tf_op jit(solution)/shard_map/all_to_all | solution.py:34
  115.0 0.6 copy.11
  115.7 3.5 %all-to-all-done.2 = bf16[128,2,4,32]{0,3,1,2:T(8,128)(2,1)S(1)} async-done(((bf16[128,2,4,32]{0,3,1,2:T(8,128)(2,1)}), bf16[128,2,4,32]{0,3,1,2:T(8,128)(2,1)S(1)}, u32[]{:S(2)}, u32[]{:S(2)}) %all-to-all-start.2) | async-done | bytes 65568 | tf_op jit(solution)/shard_map/all_to_all | solution.py:34
  119.1 3.3 %all-to-all-start.1 = ((bf16[1,32,8,128]{3,1,0,2:T(8,128)(2,1)}), bf16[1,32,8,128]{3,1,0,2:T(8,128)(2,1)S(1)}, u32[]{:S(2)}, u32[]{:S(2)}) async-start(bf16[1,32,8,128]{3,1,0,2:T(8,128)(2,1)} %bitcast.2), calls=%async_computation.1 | async-start | bytes 131072 | tf_op jit(solution)/shard_map/all_to_all | solution.py:38
  122.5 6.8 %all-to-all-done.1 = bf16[1,32,8,128]{3,1,0,2:T(8,128)(2,1)S(1)} async-done(((bf16[1,32,8,128]{3,1,0,2:T(8,128)(2,1)}), bf16[1,32,8,128]{3,1,0,2:T(8,128)(2,1)S(1)}, u32[]{:S(2)}, u32[]{:S(2)}) %all-to-all-start.1) | async-done | bytes 65568 | tf_op jit(solution)/shard_map/all_to_all | solution.py:38
  129.3 0.7 bitcast_add_fusion
  (1 shorter events, 0.0 us)
Async XLA Ops:
  6.5 28.5 %copy-start = (bf16[256,2048]{1,0:T(8,128)(2,1)S(1)}, bf16[256,2048]{1,0:T(8,128)(2,1)}, u32[]{:S(2)}) copy-start(bf16[256,2048]{1,0:T(8,128)(2,1)} %param.2) | copy-start | bytes 3145732
  6.5 85.9 %copy-start.1 = (bf16[2048,256]{1,0:T(8,128)(2,1)S(1)}, bf16[2048,256]{1,0:T(8,128)(2,1)}, u32[]{:S(2)}) copy-start(bf16[2048,256]{1,0:T(8,128)(2,1)} %param.3) | copy-start | bytes 3145732
  6.5 93.6 %all-gather.2.cloned.1.call-start = ((), (), s32[]{:S(2)}) async-start(), calls=%async_computation.3 | async-start | bytes 2621440 | tf_op jit(solution)/shard_map/all_gather | solution.py:28
  6.5 28.5 %collective-permute-start = (bf16[2048,256]{1,0:T(8,128)(2,1)}, bf16[2048,256]{1,0:T(8,128)(2,1)S(1)}, u32[]{:S(2)}, u32[]{:S(2)}) collective-permute-start(bf16[2048,256]{1,0:T(8,128)(2,1)} %param.3), channel_id=1, source_target_pairs={{0,8},{8,16},{16,24},{24,0},{1,9},{9,17},{17,25},{25,1},{2,10},{10... | collective-permute-start | bytes 3145736 | tf_op jit(solution)/shard_map/ppermute | solution.py:23
  35.0 26.2 %collective-permute-start.1 = (bf16[2048,256]{1,0:T(8,128)(2,1)S(1)}, bf16[2048,256]{1,0:T(8,128)(2,1)}, u32[]{:S(2)}, u32[]{:S(2)}) collective-permute-start(bf16[2048,256]{1,0:T(8,128)(2,1)S(1)} %collective-permute-done), channel_id=1, source_target_pairs={{0,8},{8,16},{16,24},{24,0},{1,9},{9,17},{17,25},{25,1},{2,10},{10... | collective-permute-start | bytes 3145736 | tf_op jit(solution)/shard_map/ppermute | solution.py:23
  61.2 25.6 %collective-permute-start.2 = (bf16[2048,256]{1,0:T(8,128)(2,1)}, bf16[2048,256]{1,0:T(8,128)(2,1)}, u32[]{:S(2)}, u32[]{:S(2)}) collective-permute-start(bf16[2048,256]{1,0:T(8,128)(2,1)} %collective-permute-done.1), channel_id=1, source_target_pairs={{0,8},{8,16},{16,24},{24,0},{1,9},{9,17},{17,25},{25,1},{2,10},{10... | collective-permute-start | bytes 3145736 | tf_op jit(solution)/shard_map/ppermute | solution.py:23
  104.4 7.4 %all-to-all-start = ((bf16[4,32,2,128]{3,2,1,0:T(2,128)(2,1)}), bf16[4,32,2,128]{3,2,1,0:T(2,128)(2,1)S(1)}, u32[]{:S(2)}, u32[]{:S(2)}) async-start(bf16[4,32,2,128]{3,2,1,0:T(2,128)(2,1)} %reshape.21), calls=%async_computation | async-start | bytes 131072 | tf_op jit(solution)/shard_map/all_to_all | solution.py:39
  111.7 7.4 %all-to-all-start.2 = ((bf16[128,2,4,32]{0,3,1,2:T(8,128)(2,1)}), bf16[128,2,4,32]{0,3,1,2:T(8,128)(2,1)S(1)}, u32[]{:S(2)}, u32[]{:S(2)}) async-start(bf16[128,2,4,32]{0,3,1,2:T(8,128)(2,1)} %copy.14), calls=%async_computation.2 | async-start | bytes 131072 | tf_op jit(solution)/shard_map/all_to_all | solution.py:34
  119.1 10.2 %all-to-all-start.1 = ((bf16[1,32,8,128]{3,1,0,2:T(8,128)(2,1)}), bf16[1,32,8,128]{3,1,0,2:T(8,128)(2,1)S(1)}, u32[]{:S(2)}, u32[]{:S(2)}) async-start(bf16[1,32,8,128]{3,1,0,2:T(8,128)(2,1)} %bitcast.2), calls=%async_computation.1 | async-start | bytes 131072 | tf_op jit(solution)/shard_map/all_to_all | solution.py:38
Sparse Core Ops, SparseCore 0:
  36.0 24.0 all-gather.1
